TPU v7x, 32 devices: a whole 2x2x4 slice. The times are simulated.
32 devices in a mesh: dp: 4 (over z), row: 2 (over x), col: 4 (over y, core).
Axes of the slice: x: 2, y: 2, z: 4, core: 2. Of those that a mesh axis runs over, the one named last changes fastest.
Arguments:
- images: bfloat16 [32, 729, 1152], P(('dp', 'row', 'col')), may hold values from -6 to 6
- cotangent: bfloat16 [32, 729, 1152], P(('dp', 'row', 'col')), may hold values from -6 to 6
- first_gain: float32 [1152], replicated, may hold values from 0.25 to 1.75
- first_shift: float32 [1152], replicated, may hold values from -3 to 3
- query_weight: bfloat16 [1152, 1152], P('row', 'col'), may hold values from -0.1875 to 0.1875
- query_bias: float32 [1152], P('col'), may hold values from -3 to 3
- key_weight: bfloat16 [1152, 1152], P('row', 'col'), may hold values from -0.1875 to 0.1875
- value_weight: bfloat16 [1152, 1152], P('row', 'col'), may hold values from -0.1875 to 0.1875
- value_bias: float32 [1152], P('col'), may hold values from -3 to 3
- output_weight: bfloat16 [1152, 1152], P('col', 'row'), may hold values from -0.75 to 0.75
- output_bias: float32 [1152], replicated, may hold values from -3 to 3
- second_gain: float32 [1152], replicated, may hold values from 0.1 to 1.9
- second_shift: float32 [1152], replicated, may hold values from -3 to 3
- expand_weight: bfloat16 [1152, 4304], P('row', 'col'), may hold values from -0.1875 to 0.1875
- expand_bias: float32 [4304], P('col'), may hold values from -3 to 3
- shrink_weight: bfloat16 [4304, 1152], P('col', 'row'), may hold values from -0.1875 to 0.1875
- shrink_bias: float32 [1152], replicated, may hold values from -3 to 3
Outputs:
- layer_out: bfloat16 [32, 729, 1152], P(('dp', 'row', 'col'))
- grad_images: bfloat16 [32, 729, 1152], P(('dp', 'row', 'col'))
- grad_first_gain: float32 [1152], replicated
- grad_first_shift: float32 [1152], replicated
- grad_query_weight: float32 [1152, 1152], P('row', 'col')
- grad_query_bias: float32 [1152], P('col')
- grad_key_weight: float32 [1152, 1152], P('row', 'col')
- grad_value_weight: float32 [1152, 1152], P('row', 'col')
- grad_value_bias: float32 [1152], P('col')
- grad_output_weight: float32 [1152, 1152], P('col', 'row')
- grad_output_bias: float32 [1152], replicated
- grad_second_gain: float32 [1152], replicated
- grad_second_shift: float32 [1152], replicated
- grad_expand_weight: float32 [1152, 4304], P('row', 'col')
- grad_expand_bias: float32 [4304], P('col')
- grad_shrink_weight: float32 [4304, 1152], P('col', 'row')
- grad_shrink_bias: float32 [1152], replicated
All inputs are finite; a program needn't handle non-finite values.
Results may differ from a plain program's by a relative error of at most 0.038.
Values may be sent and summed in bfloat16 or wider, within the bound.
A program may use at most 448 MiB of HBM per device.

v0:
```python
import jax
import jax.numpy as jnp
from jax import lax
from jax.sharding import PartitionSpec as P

HEAD_DIM = 72
EPS = 1e-06
contract_last = (((2,), (1,)), ((), ()))
contract_rows = (((0, 1), (0, 1)), ((), ()))


def gelu_tanh(value):
    return jax.nn.gelu(value, approximate=True)


def norm_forward(stream, gain, shift):
    average = jnp.mean(stream, axis=-1, keepdims=True)
    second = jnp.mean(stream * stream, axis=-1, keepdims=True)
    inverse = lax.rsqrt(second - average * average + EPS)
    normed = (stream - average) * inverse
    return (normed, inverse, (normed * gain + shift).astype(jnp.bfloat16))


def norm_backward(grad_out, normed, inverse, gain):
    scaled = grad_out * gain
    first = jnp.mean(scaled, axis=-1, keepdims=True)
    second = jnp.mean(scaled * normed, axis=-1, keepdims=True)
    return inverse * (scaled - first - normed * second)


def spread(block):
    feature_part = lax.all_to_all(block, "row", split_axis=2, concat_axis=0, tiled=True)
    return lax.all_gather(feature_part, "col", axis=0, tiled=True)


def join_back(summed):
    return lax.all_to_all(
        summed.astype(jnp.bfloat16), "row", split_axis=0, concat_axis=2, tiled=True
    ).astype(summed.dtype)


def project_in(normed_bf, weight):
    gathered = spread(normed_bf)
    summed = lax.psum_scatter(
        jnp.dot(gathered, weight, preferred_element_type=jnp.float32).astype(jnp.bfloat16),
        "row",
        scatter_dimension=0,
        tiled=True,
    ).astype(jnp.float32)
    return (summed, gathered)


def project_out(block_bf, weight):
    partial_sums = jnp.dot(
        lax.all_gather(block_bf, "row", axis=0, tiled=True),
        weight,
        preferred_element_type=jnp.float32,
    )
    return join_back(
        lax.psum_scatter(
            partial_sums.astype(jnp.bfloat16), "col", scatter_dimension=0, tiled=True
        ).astype(jnp.float32)
    )


def back_out(grad_bf, acts_bf, weight):
    grads_all = spread(grad_bf)
    grad_acts = lax.psum_scatter(
        lax.dot_general(
            grads_all, weight, contract_last, preferred_element_type=jnp.float32
        ).astype(jnp.bfloat16),
        "row",
        scatter_dimension=0,
        tiled=True,
    ).astype(jnp.float32)
    grad_weight = lax.dot_general(
        lax.all_gather(acts_bf, "row", axis=0, tiled=True),
        grads_all,
        contract_rows,
        preferred_element_type=jnp.float32,
    )
    return (grad_acts, grad_weight)


def back_in(grad_bf, weight, normed_bf):
    inputs_all = spread(normed_bf)
    piece = lax.all_gather(grad_bf, "row", axis=0, tiled=True)
    contrib = lax.dot_general(piece, weight, contract_last, preferred_element_type=jnp.float32)
    partial_sums = contrib
    weight_grad = lax.dot_general(
        inputs_all, piece, contract_rows, preferred_element_type=jnp.float32
    )
    partial_sums, weight_grad = (partial_sums, weight_grad)
    grad_inputs = join_back(
        lax.psum_scatter(
            partial_sums.astype(jnp.bfloat16), "col", scatter_dimension=0, tiled=True
        ).astype(jnp.float32)
    )
    return (grad_inputs, weight_grad)


def split_heads(block):
    return block.reshape(block.shape[0], block.shape[1] // HEAD_DIM, HEAD_DIM)


def head_scores(queries, key_rows):
    scores = jnp.einsum(
        "qhd,khd->hqk",
        split_heads(queries),
        split_heads(key_rows),
        preferred_element_type=jnp.float32,
    )
    return scores * HEAD_DIM ** (-0.5)


def attend(queries, key_rows, value_rows):

    def one_image(triple):
        scores = head_scores(triple[0], triple[1])
        peak = jnp.max(scores, axis=-1, keepdims=True)
        log_total = peak + jnp.log(jnp.sum(jnp.exp(scores - peak), axis=-1, keepdims=True))
        attention = jnp.exp(scores - log_total).astype(jnp.bfloat16)
        mixed = jnp.einsum(
            "hqk,khd->qhd", attention, split_heads(triple[2]), preferred_element_type=jnp.float32
        )
        return (mixed.reshape(triple[0].shape).astype(jnp.bfloat16), log_total)

    return lax.map(one_image, (queries, key_rows, value_rows))


def attend_back(queries, key_rows, value_rows, attended, log_total, grad_attended):
    scale = HEAD_DIM ** (-0.5)

    def one_image(group):
        image_q, image_k, image_v, image_out, image_total, image_grad = group
        attention = jnp.exp(head_scores(image_q, image_k) - image_total)
        grad_heads = split_heads(image_grad)
        grad_probs = jnp.einsum(
            "qhd,khd->hqk", grad_heads, split_heads(image_v), preferred_element_type=jnp.float32
        )
        delta = jnp.einsum(
            "qhd,qhd->hq", grad_heads, split_heads(image_out), preferred_element_type=jnp.float32
        )[..., None]
        grad_scores = (attention * (grad_probs - delta)).astype(jnp.bfloat16)
        grad_queries = (
            jnp.einsum(
                "hqk,khd->qhd",
                grad_scores,
                split_heads(image_k),
                preferred_element_type=jnp.float32,
            )
            * scale
        )
        grad_keys = (
            jnp.einsum(
                "hqk,qhd->khd",
                grad_scores,
                split_heads(image_q),
                preferred_element_type=jnp.float32,
            )
            * scale
        )
        grad_values = jnp.einsum(
            "hqk,qhd->khd",
            attention.astype(jnp.bfloat16),
            grad_heads,
            preferred_element_type=jnp.float32,
        )
        shape = image_q.shape
        return (grad_queries.reshape(shape), grad_keys.reshape(shape), grad_values.reshape(shape))

    return lax.map(one_image, (queries, key_rows, value_rows, attended, log_total, grad_attended))


def feature_terms(grad_input1, normed1, grad_middle, grad_input2, normed2, grad_result):
    token_axes = (0, 1)
    return (
        jnp.sum(grad_input1 * normed1, axis=token_axes),
        jnp.sum(grad_input1, axis=token_axes),
        jnp.sum(grad_middle, axis=token_axes),
        jnp.sum(grad_input2 * normed2, axis=token_axes),
        jnp.sum(grad_input2, axis=token_axes),
        jnp.sum(grad_result, axis=token_axes),
    )


def embed_part(part_sum):
    start = lax.axis_index("col") * part_sum.shape[0]
    whole = jnp.zeros((part_sum.shape[0] * lax.axis_size("col"),), jnp.float32)
    return lax.dynamic_update_slice_in_dim(whole, part_sum, start, 0)


def grid_layer(images, cotangent, params):
    (
        first_gain,
        first_shift,
        query_weight,
        query_bias,
        key_weight,
        value_weight,
        value_bias,
        output_weight,
        output_bias,
        second_gain,
        second_shift,
        expand_weight,
        expand_bias,
        shrink_weight,
        shrink_bias,
    ) = params
    width = query_weight.shape[1]
    joined = jnp.concatenate((query_weight, key_weight, value_weight), axis=1)
    stream = images.astype(jnp.float32)
    normed1, inverse1, input1 = norm_forward(stream, first_gain, first_shift)
    projected, kept_first = project_in(input1, joined)
    queries = (projected[..., :width] + query_bias).astype(jnp.bfloat16)
    key_rows = projected[..., width : 2 * width].astype(jnp.bfloat16)
    value_rows = (projected[..., 2 * width :] + value_bias).astype(jnp.bfloat16)
    attended, log_total = attend(queries, key_rows, value_rows)
    middle = stream + project_out(attended, output_weight) + output_bias
    normed2, inverse2, input2 = norm_forward(middle, second_gain, second_shift)
    expanded, kept_second = project_in(input2, expand_weight)
    before = expanded + expand_bias
    hidden = gelu_tanh(before).astype(jnp.bfloat16)
    result = middle + project_out(hidden, shrink_weight) + shrink_bias
    grad_result = cotangent.astype(jnp.float32)
    grad_hidden, grad_shrink = back_out(cotangent, hidden, shrink_weight)
    gelu_back = jax.vjp(gelu_tanh, before)[1]
    grad_before = gelu_back(grad_hidden)[0]
    grad_input2, grad_expand = back_in(grad_before.astype(jnp.bfloat16), expand_weight, input2)
    grad_middle = grad_result + norm_backward(grad_input2, normed2, inverse2, second_gain)
    grad_attended, grad_output = back_out(grad_middle.astype(jnp.bfloat16), attended, output_weight)
    grad_queries, grad_keys, grad_values = attend_back(
        queries, key_rows, value_rows, attended, log_total, grad_attended.astype(jnp.bfloat16)
    )
    grad_joined_rows = jnp.concatenate((grad_queries, grad_keys, grad_values), axis=-1).astype(
        jnp.bfloat16
    )
    grad_input1, grad_joined = back_in(grad_joined_rows, joined, input1)
    grad_stream = grad_middle + norm_backward(grad_input1, normed1, inverse1, first_gain)
    token_axes = (0, 1)
    features = feature_terms(grad_input1, normed1, grad_middle, grad_input2, normed2, grad_result)
    biases = (
        embed_part(jnp.sum(grad_queries, axis=token_axes)),
        embed_part(jnp.sum(grad_values, axis=token_axes)),
        embed_part(jnp.sum(grad_before, axis=token_axes)),
    )
    blocks = (
        grad_joined[:, :width],
        grad_joined[:, width : 2 * width],
        grad_joined[:, 2 * width :],
        grad_output,
        grad_expand,
        grad_shrink,
    )
    return (result, grad_stream, features, biases, blocks)


def shards(
    images,
    cotangent,
    first_gain,
    first_shift,
    query_weight,
    query_bias,
    key_weight,
    value_weight,
    value_bias,
    output_weight,
    output_bias,
    second_gain,
    second_shift,
    expand_weight,
    expand_bias,
    shrink_weight,
    shrink_bias,
):
    params = (
        first_gain,
        first_shift,
        query_weight,
        query_bias,
        key_weight,
        value_weight,
        value_bias,
        output_weight,
        output_bias,
        second_gain,
        second_shift,
        expand_weight,
        expand_bias,
        shrink_weight,
        shrink_bias,
    )
    result, grad_stream, features, biases, blocks = grid_layer(images, cotangent, params)
    totals = lax.psum(
        (
            features[0],
            features[1],
            features[2],
            features[3],
            features[4],
            features[5],
            biases[0],
            biases[1],
            biases[2],
        ),
        ("dp", "row", "col"),
    )
    col_index = lax.axis_index("col")
    query_part = query_bias.shape[0]
    expand_part = expand_bias.shape[0]
    query_bias_grad = lax.dynamic_slice_in_dim(totals[6], col_index * query_part, query_part, 0)
    value_bias_grad = lax.dynamic_slice_in_dim(totals[7], col_index * query_part, query_part, 0)
    expand_bias_grad = lax.dynamic_slice_in_dim(totals[8], col_index * expand_part, expand_part, 0)
    weight_totals = (
        lax.psum(blocks[0].astype(jnp.bfloat16), "dp").astype(jnp.float32),
        lax.psum(blocks[1].astype(jnp.bfloat16), "dp").astype(jnp.float32),
        lax.psum(blocks[2].astype(jnp.bfloat16), "dp").astype(jnp.float32),
        lax.psum(blocks[3].astype(jnp.bfloat16), "dp").astype(jnp.float32),
        lax.psum(blocks[4].astype(jnp.bfloat16), "dp").astype(jnp.float32),
        lax.psum(blocks[5].astype(jnp.bfloat16), "dp").astype(jnp.float32),
    )
    return (
        result.astype(jnp.bfloat16),
        grad_stream.astype(jnp.bfloat16),
        totals[0],
        totals[1],
        weight_totals[0],
        query_bias_grad,
        weight_totals[1],
        weight_totals[2],
        value_bias_grad,
        weight_totals[3],
        totals[2],
        totals[3],
        totals[4],
        weight_totals[4],
        expand_bias_grad,
        weight_totals[5],
        totals[5],
    )


def solution(mesh):
    placed = (
        P(("dp", "row", "col"), None, None),
        P(("dp", "row", "col"), None, None),
        P(),
        P(),
        P("row", "col"),
        P("col"),
        P("row", "col"),
        P("row", "col"),
        P("col"),
        P("col", "row"),
        P(),
        P(),
        P(),
        P("row", "col"),
        P("col"),
        P("col", "row"),
        P(),
    )
    return jax.shard_map(
        shards,
        mesh=mesh,
        in_specs=placed,
        out_specs=(
            P(("dp", "row", "col"), None, None),
            P(("dp", "row", "col"), None, None),
            P(),
            P(),
            P("row", "col"),
            P("col"),
            P("row", "col"),
            P("row", "col"),
            P("col"),
            P("col", "row"),
            P(),
            P(),
            P(),
            P("row", "col"),
            P("col"),
            P("col", "row"),
            P(),
        ),
        check_vma=False,
    )
```

profile of v0, /device:TPU:0, one launch (start us, length us, event | category | flops | bytes accessed | tf_op | source)
XLA Modules:
  0.0 2109.9 jit_solution(17329852611036355849)
XLA Ops:
  12.2 7.6 copy.176
  20.3 11.7 reduce.14
  32.0 5.9 reshape.487
  37.9 25.5 %all_to_all.118 = bf16[2,2,209952]{2,1,0:T(2,128)(2,1)S(1)} all-to-all(bf16[2,2,209952]{2,1,0:T(2,128)(2,1)} %reshape.487), channel_id=1, replica_groups=mesh['dp'=4,'row'=2,'col'=4] {'row'}, dimensions={0} | all-to-all | bytes 3359232 | tf_op jit(solution)/shard_map/all_to_all | solution.py:32
  63.5 5.7 reshape.488
  74.0 50.2 %all-gather.21.cloned.1.call-done = bf16[8,1,729,576]{2,3,1,0:T(8,128)(2,1)} async-done(((bf16[2,1,729,576]{2,3,1,0:T(8,128)(2,1)}), bf16[8,1,729,576]{2,3,1,0:T(8,128)(2,1)}) %all-gather.21.cloned.1.call-update) | async-done | bytes 6718480 | tf_op jit(solution)/shard_map/all_gather | solution.py:33
  124.3 14.3 fusion.37
  138.8 122.5 %reduce-scatter.9.cloned.1.call-done = bf16[4,729,864]{2,1,0:T(8,128)(2,1)} async-done(((bf16[8,729,864]{2,1,0:T(8,128)(2,1)}), bf16[4,729,864]{2,1,0:T(8,128)(2,1)}) %reduce-scatter.9.cloned.1.call-update) | async-done | bytes 5038864 | tf_op jit(solution)/shard_map/reduce_scatter | solution.py:44
  261.4 4.4 slice.30
  275.4 4.1 copy.182
  283.5 32.8 %while.26 = (s32[]{:T(128)}, bf16[4,729,288]{1,2,0:T(8,128)(2,1)}, f32[4,4,729,1]{2,1,3,0:T(4,128)}, bf16[4,729,288]{1,2,0:T(8,128)(2,1)}, bf16[4,729,288]{1,2,0...) while((s32[]{:T(128)}, bf16[4,729,288]{1,2,0:T(8,128)(2,1)}, f32[4,4,729,1]{2,1,3,0:T(4,128)}, ...), condition=%wide.region_6.7_spmd, body=%wide.region_3.6_spmd.sunk | while | flops 629433152 | bytes 30664516 | solution.py:128
  316.6 49.3 %all-gather.13.cloned.1.call-done = bf16[8,729,288]{1,2,0:T(8,128)(2,1)} async-done(((bf16[4,729,288]{1,2,0:T(8,128)(2,1)}), bf16[8,729,288]{1,2,0:T(8,128)(2,1)}) %all-gather.13.cloned.1.call-update) | async-done | bytes 3359248 | tf_op jit(solution)/shard_map/all_gather | solution.py:55
  365.9 8.8 convolution_convert_fusion.5
  376.1 7.5 copy.188
  383.6 11.9 reduce.16
  395.6 5.9 reshape.489
  401.5 24.2 %all_to_all.119 = bf16[2,2,209952]{2,1,0:T(2,128)(2,1)S(1)} all-to-all(bf16[2,2,209952]{2,1,0:T(2,128)(2,1)} %reshape.489), channel_id=1, replica_groups=mesh['dp'=4,'row'=2,'col'=4] {'row'}, dimensions={0} | all-to-all | bytes 3359232 | tf_op jit(solution)/shard_map/all_to_all | solution.py:32
  425.6 5.6 reshape.490
  434.8 4.2 reduce-scatter.11.cloned.1.call-done
  439.0 25.5 %all_to_all.120 = bf16[2,729,576]{1,2,0:T(8,128)(2,1)S(1)} all-to-all(bf16[2,729,576]{1,2,0:T(8,128)(2,1)} %reduce-scatter.11.cloned.1.call-done), channel_id=1, replica_groups=mesh['dp'=4,'row'=2,'col'=4] {'row'}, dimensions={0} | all-to-all | bytes 3359232 | tf_op jit(solution)/shard_map/all_to_all | solution.py:37
  466.6 5.3 copy.184
  477.1 7.6 copy.185
  484.6 11.8 reduce.15
  496.4 5.9 reshape.491
  502.3 23.4 %all_to_all.121 = bf16[2,2,209952]{2,1,0:T(2,128)(2,1)S(1)} all-to-all(bf16[2,2,209952]{2,1,0:T(2,128)(2,1)} %reshape.491), channel_id=1, replica_groups=mesh['dp'=4,'row'=2,'col'=4] {'row'}, dimensions={0} | all-to-all | bytes 3359232 | tf_op jit(solution)/shard_map/all_to_all | solution.py:32
  525.7 5.7 reshape.492
  535.3 16.6 convolution_convert_fusion
  551.9 33.1 %all-gather.23.cloned.1.call-done = bf16[8,1,729,576]{2,3,1,0:T(8,128)(2,1)} async-done(((bf16[2,1,729,576]{2,3,1,0:T(8,128)(2,1)}), bf16[8,1,729,576]{2,3,1,0:T(8,128)(2,1)}) %all-gather.23.cloned.1.call-update) | async-done | bytes 6718480 | tf_op jit(solution)/shard_map/all_gather | solution.py:33
  585.1 16.6 convolution_convert_fusion.1
  601.7 137.7 %reduce-scatter.17.cloned.1.call-done = bf16[4,729,1076]{1,2,0:T(8,128)(2,1)} async-done(((bf16[8,729,1076]{1,2,0:T(8,128)(2,1)}), bf16[4,729,1076]{1,2,0:T(8,128)(2,1)}) %reduce-scatter.17.cloned.1.call-update) | async-done | bytes 6275248 | tf_op jit(solution)/shard_map/reduce_scatter | solution.py:68
  739.4 154.3 %reduce-scatter.13.cloned.1.call-done = bf16[4,729,1076]{1,2,0:T(8,128)(2,1)} async-done(((bf16[8,729,1076]{1,2,0:T(8,128)(2,1)}), bf16[4,729,1076]{1,2,0:T(8,128)(2,1)}) %reduce-scatter.13.cloned.1.call-update) | async-done | bytes 6275248 | tf_op jit(solution)/shard_map/reduce_scatter | solution.py:44
  893.7 17.1 fusion.91
  911.7 159.4 %all-gather.17.cloned.1.call-done = bf16[8,729,1076]{1,2,0:T(8,128)(2,1)} async-done(((bf16[4,729,1076]{1,2,0:T(8,128)(2,1)}), bf16[8,729,1076]{1,2,0:T(8,128)(2,1)}) %all-gather.17.cloned.1.call-update) | async-done | bytes 12550480 | tf_op jit(solution)/shard_map/all_gather | solution.py:87
  1071.0 15.9 convolution_convert_fusion.2
  1087.0 145.5 %all-gather.15.cloned.1.call-done = bf16[8,729,1076]{1,2,0:T(8,128)(2,1)} async-done(((bf16[4,729,1076]{1,2,0:T(8,128)(2,1)}), bf16[8,729,1076]{1,2,0:T(8,128)(2,1)}) %all-gather.15.cloned.1.call-update) | async-done | bytes 12550480 | tf_op jit(solution)/shard_map/all_gather | solution.py:55
  1232.5 15.9 convolution_convert_fusion.3
  1248.4 50.8 %reduce-scatter.19.cloned.1.call-done = bf16[2,729,576]{1,2,0:T(8,128)(2,1)} async-done(((bf16[8,729,576]{1,2,0:T(8,128)(2,1)}), bf16[2,729,576]{1,2,0:T(8,128)(2,1)}) %reduce-scatter.19.cloned.1.call-update) | async-done | bytes 1679632 | tf_op jit(solution)/shard_map/reduce_scatter | solution.py:95
  1303.1 62.8 %reduce-scatter.15.cloned.1.call-done = bf16[2,729,576]{1,2,0:T(8,128)(2,1)} async-done(((bf16[8,729,576]{1,2,0:T(8,128)(2,1)}), bf16[2,729,576]{1,2,0:T(8,128)(2,1)}) %reduce-scatter.15.cloned.1.call-update) | async-done | bytes 1679632 | tf_op jit(solution)/shard_map/reduce_scatter | solution.py:60
  1365.9 4.7 all-to-all-start.3
  1373.2 5.3 copy.190
  1385.0 7.1 all-to-all-done.3
  1395.6 5.2 copy.187
  1400.8 6.5 fusion.93
  1410.7 8.9 copy.191
  1419.6 11.9 reduce.17
  1431.5 6.2 reshape.493
  1437.7 23.0 %all_to_all.122 = bf16[2,2,209952]{2,1,0:T(2,128)(2,1)} all-to-all(bf16[2,2,209952]{2,1,0:T(2,128)(2,1)S(1)} %reshape.493), channel_id=1, replica_groups=mesh['dp'=4,'row'=2,'col'=4] {'row'}, dimensions={0} | all-to-all | bytes 3359232 | tf_op jit(solution)/shard_map/all_to_all | solution.py:32
  1460.6 5.6 reshape.494
  1468.0 49.9 %all-gather.27.cloned.1.call-done = bf16[8,1,729,576]{2,3,1,0:T(8,128)(2,1)} async-done(((bf16[2,1,729,576]{2,3,1,0:T(8,128)(2,1)}), bf16[8,1,729,576]{2,3,1,0:T(8,128)(2,1)}) %all-gather.27.cloned.1.call-update) | async-done | bytes 6718480 | tf_op jit(solution)/shard_map/all_gather | solution.py:33
  1517.9 7.7 fusion.71
  1525.7 47.8 %reduce-scatter.21.cloned.1.call-done = bf16[4,729,288]{1,2,0:T(8,128)(2,1)} async-done(((bf16[8,729,288]{1,2,0:T(8,128)(2,1)}), bf16[4,729,288]{1,2,0:T(8,128)(2,1)}) %reduce-scatter.21.cloned.1.call-update) | async-done | bytes 1679632 | tf_op jit(solution)/shard_map/reduce_scatter | solution.py:68
  1573.5 70.2 %while.27 = (s32[]{:T(128)}, f32[4,729,288]{1,2,0:T(8,128)}, bf16[4,729,288]{1,2,0:T(8,128)(2,1)}, f32[4,729,288]{1,2,0:T(8,128)S(1)}, bf16[4,729,288]{1,2,0:T(8...) while((s32[]{:T(128)}, f32[4,729,288]{1,2,0:T(8,128)}, ...), condition=%wide.region_18.19_spmd, body=%wide.region_17.18_spmd.sunk | while | flops 1549022848 | bytes 52812796 | solution.py:172
  1651.1 8.0 copy.196
  1659.2 130.3 %all-gather.19.cloned.1.call-done = bf16[8,729,864]{2,1,0:T(8,128)(2,1)} async-done(((bf16[4,729,864]{2,1,0:T(8,128)(2,1)}), bf16[8,729,864]{2,1,0:T(8,128)(2,1)}) %all-gather.19.cloned.1.call-update) | async-done | bytes 10077712 | tf_op jit(solution)/shard_map/all_gather | solution.py:87
  1789.5 13.6 convolution_convert_fusion.4
  1803.2 14.9 fusion.68
  1818.0 15.1 fusion.65
  1833.1 7.8 fusion.83
  1840.9 10.2 bitcast_convert_fusion
  1852.6 14.8 reduce-scatter.23.cloned.1.call-done
  1872.1 159.5 %all-reduce.4.cloned.1.call-done = (bf16[576,288]{1,0:T(8,128)(2,1)}, bf16[576,288]{1,0:T(8,128)(2,1)}, bf16[576,288]{1,0:T(8,128)(2,1)}, bf16[288,576]{1,0:T(8,...) async-done(((bf16[576,288]{1,0:T(8,128)(2,1)}, bf16[576,288]{1,0:T(8,128)(2,1)}, bf16[576,288]{1,0:T(8,128)(2,1)}, bf16[288,576]{1,0:T(8,128)(2,1)}, ...) | async-done | bytes 3806224 | tf_op jit(solution)/shard_map/psum | solution.py:317
  2046.6 5.3 copy.197
  2055.0 41.5 %all-reduce = (f32[1152]{0:T(1024)}, f32[1152]{0:T(1024)}, f32[1152]{0:T(1024)S(1)}, f32[1152]{0:T(1024)S(1)}, f32[1152]{0:T(1024)}, /*index=5*/f32[1152]{0:T(10...) all-reduce(f32[1152]{0:T(1024)S(1)} %get-tuple-element.309, ...), channel_id=1, replica_groups=mesh['dp'=4,'row'=2,'col'=4] {'dp','row','col'}, use_global_device_ids=true, to_apply=%region_23.24 | all-reduce | flops 13520 | bytes 108160 | tf_op jit(solution)/shard_map/psum | solution.py:296
  2098.5 4.5 fusion.55
  (268 shorter events, 199.3 us)
Async XLA Ops:
  7.2 577.9 %copy-start = (bf16[576,1076]{1,0:T(8,128)(2,1)S(1)}, bf16[576,1076]{1,0:T(8,128)(2,1)}, u32[]{:S(2)}) copy-start(bf16[576,1076]{1,0:T(8,128)(2,1)} %param.34) | copy-start | bytes 3718660
  7.2 117.1 %all-gather.21.cloned.1.call-start = ((), (), s32[]{:S(2)}) async-start(), calls=%async_computation.28 | async-start | bytes 8847360 | tf_op jit(solution)/shard_map/all_gather | solution.py:33
  9.4 0.6 copy-start.23
  9.4 0.6 copy-start.25
  69.1 4.1 copy-start.17
  69.1 4.4 copy-start.18
  69.1 4.7 copy-start.19
  72.7 188.6 %reduce-scatter.9.cloned.1.call-start = ((), (), s32[]{:S(2)}) async-start(), calls=%async_computation.16 | async-start | bytes 15826944 | tf_op jit(solution)/shard_map/reduce_scatter | solution.py:44
  73.5 65.0 %copy-start.11 = (bf16[576,288]{1,0:T(8,128)(2,1)}, bf16[576,288]{1,0:T(8,128)(2,1)S(1)}, u32[]{:S(2)}) copy-start(bf16[576,288]{1,0:T(8,128)(2,1)S(1)} %copy.178) | copy-start | bytes 995332
  73.8 64.8 %copy-start.13 = (bf16[576,288]{1,0:T(8,128)(2,1)}, bf16[576,288]{1,0:T(8,128)(2,1)S(1)}, u32[]{:S(2)}) copy-start(bf16[576,288]{1,0:T(8,128)(2,1)S(1)} %copy.179) | copy-start | bytes 995332
  74.0 64.5 %copy-start.15 = (bf16[576,288]{1,0:T(8,128)(2,1)}, bf16[576,288]{1,0:T(8,128)(2,1)S(1)}, u32[]{:S(2)}) copy-start(bf16[576,288]{1,0:T(8,128)(2,1)S(1)} %copy.180) | copy-start | bytes 995332
  138.6 227.3 %all-gather.13.cloned.1.call-start = ((), (), s32[]{:S(2)}) async-start(), calls=%async_computation.17 | async-start | bytes 5308416 | tf_op jit(solution)/shard_map/all_gather | solution.py:55
  268.7 3.2 copy-start.36
  268.7 3.2 copy-start.37
  283.5 82.4 %copy-start.39 = (bf16[288,576]{1,0:T(8,128)(2,1)S(1)}, bf16[288,576]{1,0:T(8,128)(2,1)}, u32[]{:S(2)}) copy-start(bf16[288,576]{1,0:T(8,128)(2,1)} %param.30) | copy-start | bytes 995332
  316.3 58.4 %copy-start.6 = (bf16[4,729,288]{1,2,0:T(8,128)(2,1)}, bf16[4,729,288]{1,2,0:T(8,128)(2,1)S(1)}, u32[]{:S(2)}) copy-start(bf16[4,729,288]{1,2,0:T(8,128)(2,1)S(1)} %get-tuple-element.600) | copy-start | bytes 5038852
  316.3 122.7 %reduce-scatter.11.cloned.1.call-start = ((), (), s32[]{:S(2)}) async-start(), calls=%async_computation.18 | async-start | bytes 8847360 | tf_op jit(solution)/shard_map/reduce_scatter | solution.py:60
  374.7 1.5 copy-start.8
  374.7 160.6 %all-gather.25.cloned.1.call-start = ((), (), s32[]{:S(2)}) async-start(), calls=%async_computation.30 | async-start | bytes 8847360 | tf_op jit(solution)/shard_map/all_gather | solution.py:33
  434.8 150.3 %all-gather.23.cloned.1.call-start = ((), (), s32[]{:S(2)}) async-start(), calls=%async_computation.29 | async-start | bytes 8847360 | tf_op jit(solution)/shard_map/all_gather | solution.py:33
  466.6 5.3 copy-start.4
  466.6 5.3 copy-start.32
  472.0 4.5 copy-start.21
  472.0 4.5 copy-start.33
  474.7 1.8 copy-start.2
  531.4 3.9 copy-start.38
  535.0 204.4 %reduce-scatter.17.cloned.1.call-start = ((), (), s32[]{:S(2)}) async-start(), calls=%async_computation.22 | async-start | bytes 19906560 | tf_op jit(solution)/shard_map/reduce_scatter | solution.py:68
  551.9 341.8 %reduce-scatter.13.cloned.1.call-start = ((), (), s32[]{:S(2)}) async-start(), calls=%async_computation.19 | async-start | bytes 19906560 | tf_op jit(solution)/shard_map/reduce_scatter | solution.py:44
  601.6 292.0 %copy-start.34 = (f32[1076]{0:T(1024)S(1)}, f32[1076]{0:T(1024)}, u32[]{:S(2)}) copy-start(f32[1076]{0:T(1024)} %param.35) | copy-start | bytes 12916
  601.7 469.4 %all-gather.17.cloned.1.call-start = ((), (), s32[]{:S(2)}) async-start(), calls=%async_computation.23 | async-start | bytes 19906560 | tf_op jit(solution)/shard_map/all_gather | solution.py:87
  910.8 321.7 %all-gather.15.cloned.1.call-start = ((), (), s32[]{:S(2)}) async-start(), calls=%async_computation.20 | async-start | bytes 19906560 | tf_op jit(solution)/shard_map/all_gather | solution.py:55
  911.4 387.9 %reduce-scatter.19.cloned.1.call-start = ((), (), s32[]{:S(2)}) async-start(), calls=%async_computation.24 | async-start | bytes 8847360 | tf_op jit(solution)/shard_map/reduce_scatter | solution.py:95
  1086.9 279.0 %reduce-scatter.15.cloned.1.call-start = ((), (), s32[]{:S(2)}) async-start(), calls=%async_computation.21 | async-start | bytes 8847360 | tf_op jit(solution)/shard_map/reduce_scatter | solution.py:60
  1299.3 66.6 %all-to-all-start.5 = ((bf16[2,729,576]{1,2,0:T(8,128)(2,1)}), bf16[2,729,576]{1,2,0:T(8,128)(2,1)S(1)}, u32[]{:S(2)}, u32[]{:S(2)}) async-start(bf16[2,729,576]{1,2,0:T(8,128)(2,1)} %reduce-scatter.19.cloned.1.call-done), calls=%async_computation.11 | async-start | bytes 3538944 | tf_op jit(solution)/shard_map/all_to_all | solution.py:37
  1365.9 7.2 copy-start.7
  1365.9 26.2 %all-to-all-start.3 = ((bf16[2,729,576]{1,2,0:T(8,128)(2,1)}), bf16[2,729,576]{1,2,0:T(8,128)(2,1)}, u32[]{:S(2)}, u32[]{:S(2)}) async-start(bf16[2,729,576]{1,2,0:T(8,128)(2,1)} %reduce-scatter.15.cloned.1.call-done), calls=%async_computation.7 | async-start | bytes 3538944 | tf_op jit(solution)/shard_map/all_to_all | solution.py:37
  1370.6 147.3 %all-gather.27.cloned.1.call-start = ((), (), s32[]{:S(2)}) async-start(), calls=%async_computation.31 | async-start | bytes 8847360 | tf_op jit(solution)/shard_map/all_gather | solution.py:33
  1373.1 8.3 copy-start.3
  1395.6 5.2 copy-start.35
  1467.8 105.7 %reduce-scatter.21.cloned.1.call-start = ((), (), s32[]{:S(2)}) async-start(), calls=%async_computation.25 | async-start | bytes 5308416 | tf_op jit(solution)/shard_map/reduce_scatter | solution.py:68
  1525.6 263.9 %all-gather.19.cloned.1.call-start = ((), (), s32[]{:S(2)}) async-start(), calls=%async_computation.26 | async-start | bytes 15826944 | tf_op jit(solution)/shard_map/all_gather | solution.py:87
  1643.7 3.9 copy-start.9
  1659.1 130.4 %copy-start.12 = (bf16[576,288]{1,0:T(8,128)(2,1)S(1)}, bf16[576,288]{1,0:T(8,128)(2,1)}, u32[]{:S(2)}) copy-start(bf16[576,288]{1,0:T(8,128)(2,1)} %copy-done.11) | copy-start | bytes 995332
  1659.1 130.4 %copy-start.14 = (bf16[576,288]{1,0:T(8,128)(2,1)S(1)}, bf16[576,288]{1,0:T(8,128)(2,1)}, u32[]{:S(2)}) copy-start(bf16[576,288]{1,0:T(8,128)(2,1)} %copy-done.13) | copy-start | bytes 995332
  1659.1 130.4 %copy-start.16 = (bf16[576,288]{1,0:T(8,128)(2,1)S(1)}, bf16[576,288]{1,0:T(8,128)(2,1)}, u32[]{:S(2)}) copy-start(bf16[576,288]{1,0:T(8,128)(2,1)} %copy-done.15) | copy-start | bytes 995332
  1659.1 208.3 %reduce-scatter.23.cloned.1.call-start = ((), (), s32[]{:S(2)}) async-start(), calls=%async_computation.27 | async-start | bytes 8847360 | tf_op jit(solution)/shard_map/reduce_scatter | solution.py:95
  1803.1 228.5 %all-reduce.4.cloned.1.call-start = ((), (), s32[]{:S(2)}) async-start(), calls=%async_computation.32 | async-start | bytes 8699904 | tf_op jit(solution)/shard_map/psum | solution.py:317
  1803.1 37.8 %slice-start = ((s8[10551296]{0:T(1024)(128)(4,1)}), s8[4194304]{0:T(1024)(128)(4,1)S(1)}, s32[]{:S(2)}) async-start(s8[10551296]{0:T(1024)(128)(4,1)} %bitcast.269), calls=%async_computation.33 | async-start | bytes 8388608
  1803.1 37.8 %slice-start.1 = ((s8[10551296]{0:T(1024)(128)(4,1)}), s8[4194304]{0:T(1024)(128)(4,1)S(1)}, s32[]{:S(2)}) async-start(s8[10551296]{0:T(1024)(128)(4,1)} %bitcast.269), calls=%async_computation.34 | async-start | bytes 8388608
  1818.0 22.9 %slice-start.2 = ((s8[10551296]{0:T(1024)(128)(4,1)}), s8[2162688]{0:T(1024)(128)(4,1)S(1)}, s32[]{:S(2)}) async-start(s8[10551296]{0:T(1024)(128)(4,1)} %bitcast.269), calls=%async_computation.35 | async-start | bytes 4325376
  1852.6 18.6 copy-start.22
  1852.6 18.7 copy-start.27
  1852.6 19.0 copy-start.31
  1867.4 176.1 %all-to-all-start.7 = ((bf16[2,729,576]{1,2,0:T(8,128)(2,1)}), bf16[2,729,576]{1,2,0:T(8,128)(2,1)S(1)}, u32[]{:S(2)}, u32[]{:S(2)}) async-start(bf16[2,729,576]{1,2,0:T(8,128)(2,1)} %reduce-scatter.23.cloned.1.call-done), calls=%async_computation.15 | async-start | bytes 3538944 | tf_op jit(solution)/shard_map/all_to_all | solution.py:37
  2031.6 6.3 copy-start.20
  2033.7 8.1 copy-start.10
  2046.6 5.3 copy-start.5
  2046.6 5.3 copy-start.24
  2046.6 5.3 copy-start.26
  2051.9 3.1 copy-start.28
  2051.9 3.1 copy-start.29
  2051.9 3.1 copy-start.30
  2097.8 5.2 copy-start.1
Sparse Core Ops, SparseCore 0:
  72.9 51.3 all-gather.20
  138.7 122.6 reduce-scatter.8
  316.5 49.3 all-gather.12
  374.8 64.1 reduce-scatter.10
  440.5 50.8 all-gather.24
  535.1 49.8 all-gather.22
  587.4 151.9 reduce-scatter.16
  741.7 151.9 reduce-scatter.12
  910.9 160.0 all-gather.16
  1072.4 160.0 all-gather.14
  1235.0 64.1 reduce-scatter.18
  1301.7 64.1 reduce-scatter.14
  1467.9 49.9 all-gather.26
  1525.7 47.7 reduce-scatter.20
  1659.2 130.1 all-gather.18
  1803.2 64.1 reduce-scatter.22
  1871.3 160.2 all-reduce.3
where the time goes:
time: 2120 us; the launch traced here: 2110 us
  waiting for transfers between devices  1380 us (65%)
  matrix products  208 us (10%)
  local copies, waits for them, and re-layouts  194 us (9%)
  blocking collectives  163 us (8%)
  other arithmetic  135 us (6%)
    all_gather x2, waiting for transfers between devices, back_in(): piece = lax.all_gather(grad_bf, 'row', axis=0, tiled=True)  290 us
    reduce_scatter x2, waiting for transfers between devices, project_in(): lax.psum_scatter(jnp.dot(gathered, weight, preferred_element_type=jnp.flo...  277 us
    all_gather x2, waiting for transfers between devices, project_out(): lax.all_gather(block_bf, 'row', axis=0, tiled=True)  195 us
    reduce_scatter x2, waiting for transfers between devices, back_out(): lax.psum_scatter(lax.dot_general(grads_all, weight, contract_last, prefer...  185 us
    psum x1, waiting for transfers between devices, shards(): lax.psum(blocks[0].astype(jnp.bfloat16), 'dp').astype(jnp.float32)  159 us
    all_gather x4, waiting for transfers between devices, spread(): return lax.all_gather(feature_part, 'col', axis=0, tiled=True)  133 us
    all_to_all x4, blocking collectives, spread(): lax.all_to_all(block, 'row', split_axis=2, concat_axis=0, tiled=True)  96.1 us
    unnamed x106, local copies, waits for them, and re-layouts  77.6 us
  transfers between devices with their start and end apart: 20, of which 17 were waited for; matrix products, arithmetic and copies ran while one was open for 11% of the time, Pallas kernels for 0%

commit v1 on v0

--- a/solution.py
+++ b/solution.py
@@ -2,6 +2,7 @@
 import jax.numpy as jnp
 from jax import lax
 from jax.sharding import PartitionSpec as P
+from jax.lax import all_to_all, psum
 
 HEAD_DIM = 72
 EPS = 1e-06
@@ -29,7 +30,9 @@
 
 
 def spread(block):
-    feature_part = lax.all_to_all(block, "row", split_axis=2, concat_axis=0, tiled=True)
+    o_now = jnp.split(block, psum(1, axis_name="row"), axis=2)
+    k_now = all_to_all(jnp.stack(o_now, 0), concat_axis=0, split_axis=0, axis_name="row")
+    feature_part = jnp.concatenate(k_now, 0)
     return lax.all_gather(feature_part, "col", axis=0, tiled=True)
 
 

time: 2120 us -> 2000 us (0.943)
  local copies, waits for them, and re-layouts: 194 us -> 103 us
  other arithmetic: 135 us -> 73.1 us
  waiting for transfers between devices: 1380 us -> 1410 us
    unnamed x106 -> x98, local copies, waits for them, and re-layouts: 77.6 us -> 28.2 us
    unnamed x5 -> x1, other arithmetic: 47.3 us -> 0.01 us
    convert_element_type x7 -> x0, local copies, waits for them, and re-layouts: 45.2 us -> none  [the longest x4 21.1 us: join_back(): return lax.all_to_all(summed.astype(jnp.bfloat16), 'row', split_axis=0, c...]
    reduce_scatter x2, waiting for transfers between devices: 67 us -> 95.1 us  [project_out(): lax.psum_scatter(partial_sums.astype(jnp.bfloat16), 'col', scatter_dimens...]
  transfers between devices with their start and end apart: 20 -> 20, of which waited for: 17 -> 17; matrix products, arithmetic and copies ran while one was open for 11% -> 7% of each run, Pallas kernels for 0% -> 0%
where the time goes in v1:
time: 2000 us; the launch traced here: 1990 us
  waiting for transfers between devices  1410 us (70%)
  matrix products  208 us (10%)
  blocking collectives  166 us (8%)
  local copies, waits for them, and re-layouts  103 us (5%)
  other arithmetic  73.1 us (4%)
    all_gather x2, waiting for transfers between devices, back_in(): piece = lax.all_gather(grad_bf, 'row', axis=0, tiled=True)  290 us
    reduce_scatter x2, waiting for transfers between devices, project_in(): lax.psum_scatter(jnp.dot(gathered, weight, preferred_element_type=jnp.flo...  277 us
    all_gather x2, waiting for transfers between devices, project_out(): lax.all_gather(block_bf, 'row', axis=0, tiled=True)  194 us
    reduce_scatter x2, waiting for transfers between devices, back_out(): lax.psum_scatter(lax.dot_general(grads_all, weight, contract_last, prefer...  185 us
    psum x1, waiting for transfers between devices, shards(): lax.psum(blocks[0].astype(jnp.bfloat16), 'dp').astype(jnp.float32)  156 us
    all_gather x4, waiting for transfers between devices, spread(): return lax.all_gather(feature_part, 'col', axis=0, tiled=True)  131 us
    all_to_all x4, blocking collectives, spread(): all_to_all(jnp.stack(o_now, 0), concat_axis=0, split_axis=0, axis_name='r...  99.2 us
    reduce_scatter x2, waiting for transfers between devices, project_out(): lax.psum_scatter(partial_sums.astype(jnp.bfloat16), 'col', scatter_dimens...  95.1 us
  transfers between devices with their start and end apart: 20, of which 17 were waited for; matrix products, arithmetic and copies ran while one was open for 7% of the time, Pallas kernels for 0%

profile of v1, /device:TPU:0, one launch (start us, length us, event | category | flops | bytes accessed | tf_op | source)
XLA Modules:
  0.0 1990.5 jit_solution(3591952807556114953)
XLA Ops:
  7.3 2.7 copy.104
  12.1 26.2 %all_to_all.58 = bf16[2,1,729,576]{2,3,1,0:T(8,128)(2,1)} all-to-all(bf16[2,1,729,576]{2,3,1,0:T(8,128)(2,1)S(1)} %pad_maximum_fusion.1), channel_id=1, replica_groups=mesh['dp'=4,'row'=2,'col'=4] {'row'}, dimensions={0} | all-to-all | bytes 3359232 | tf_op jit(solution)/shard_map/all_to_all | solution.py:34
  43.7 46.2 %all-gather.21.cloned.1.call-done = bf16[8,1,729,576]{2,3,1,0:T(8,128)(2,1)} async-done(((bf16[2,1,729,576]{2,3,1,0:T(8,128)(2,1)}), bf16[8,1,729,576]{2,3,1,0:T(8,128)(2,1)}) %all-gather.21.cloned.1.call-update) | async-done | bytes 6718480 | tf_op jit(solution)/shard_map/all_gather | solution.py:36
  89.9 14.6 fusion.37
  105.1 122.2 %reduce-scatter.9.cloned.1.call-done = bf16[4,729,864]{2,1,0:T(8,128)(2,1)} async-done(((bf16[8,729,864]{2,1,0:T(8,128)(2,1)}), bf16[4,729,864]{2,1,0:T(8,128)(2,1)}) %reduce-scatter.9.cloned.1.call-update) | async-done | bytes 5038864 | tf_op jit(solution)/shard_map/reduce_scatter | solution.py:47
  227.3 4.4 slice.30
  231.7 4.1 copy.110
  235.8 3.2 convert_element_type.244
  239.0 3.4 fusion.40
  242.4 4.1 copy.109
  246.5 4.0 copy.108
  250.5 33.4 %while.26 = (s32[]{:T(128)}, bf16[4,729,288]{1,2,0:T(8,128)(2,1)}, f32[4,4,729,1]{2,1,3,0:T(4,128)}, bf16[4,729,288]{1,2,0:T(8,128)(2,1)}, bf16[4,729,288]{1,2,0...) while((s32[]{:T(128)}, bf16[4,729,288]{1,2,0:T(8,128)(2,1)}, f32[4,4,729,1]{2,1,3,0:T(4,128)}, ...), condition=%wide.region_6.7_spmd, body=%wide.region_3.6_spmd.sunk | while | flops 629433152 | bytes 30664516 | solution.py:131
  284.1 49.3 %all-gather.13.cloned.1.call-done = bf16[8,729,288]{1,2,0:T(8,128)(2,1)} async-done(((bf16[4,729,288]{1,2,0:T(8,128)(2,1)}), bf16[8,729,288]{1,2,0:T(8,128)(2,1)}) %all-gather.13.cloned.1.call-update) | async-done | bytes 3359248 | tf_op jit(solution)/shard_map/all_gather | solution.py:58
  333.4 8.8 convolution_convert_fusion.5
  342.3 3.8 copy.111
  347.8 24.8 %all_to_all.59 = bf16[2,1,729,576]{2,3,1,0:T(8,128)(2,1)} all-to-all(bf16[2,1,729,576]{2,3,1,0:T(8,128)(2,1)S(1)} %pad_maximum_fusion.3), channel_id=1, replica_groups=mesh['dp'=4,'row'=2,'col'=4] {'row'}, dimensions={0} | all-to-all | bytes 3359232 | tf_op jit(solution)/shard_map/all_to_all | solution.py:34
  372.7 33.9 %reduce-scatter.11.cloned.1.call-done = bf16[2,729,576]{1,2,0:T(8,128)(2,1)} async-done(((bf16[8,729,576]{1,2,0:T(8,128)(2,1)}), bf16[2,729,576]{1,2,0:T(8,128)(2,1)}) %reduce-scatter.11.cloned.1.call-update) | async-done | bytes 1679632 | tf_op jit(solution)/shard_map/reduce_scatter | solution.py:63
  406.6 25.1 %all_to_all.60 = bf16[2,729,576]{1,2,0:T(8,128)(2,1)S(1)} all-to-all(bf16[2,729,576]{1,2,0:T(8,128)(2,1)} %reduce-scatter.11.cloned.1.call-done), channel_id=1, replica_groups=mesh['dp'=4,'row'=2,'col'=4] {'row'}, dimensions={0} | all-to-all | bytes 3359232 | tf_op jit(solution)/shard_map/all_to_all | solution.py:40
  435.1 24.2 %all_to_all.61 = bf16[2,1,729,576]{2,3,1,0:T(8,128)(2,1)} all-to-all(bf16[2,1,729,576]{2,3,1,0:T(8,128)(2,1)S(1)} %pad_maximum_fusion.2), channel_id=1, replica_groups=mesh['dp'=4,'row'=2,'col'=4] {'row'}, dimensions={0} | all-to-all | bytes 3359232 | tf_op jit(solution)/shard_map/all_to_all | solution.py:34
  459.4 16.6 convolution_convert_fusion
  476.3 34.9 %all-gather.23.cloned.1.call-done = bf16[8,1,729,576]{2,3,1,0:T(8,128)(2,1)} async-done(((bf16[2,1,729,576]{2,3,1,0:T(8,128)(2,1)}), bf16[8,1,729,576]{2,3,1,0:T(8,128)(2,1)}) %all-gather.23.cloned.1.call-update) | async-done | bytes 6718480 | tf_op jit(solution)/shard_map/all_gather | solution.py:36
  511.2 16.6 convolution_convert_fusion.1
  527.8 137.6 %reduce-scatter.17.cloned.1.call-done = bf16[4,729,1076]{1,2,0:T(8,128)(2,1)} async-done(((bf16[8,729,1076]{1,2,0:T(8,128)(2,1)}), bf16[4,729,1076]{1,2,0:T(8,128)(2,1)}) %reduce-scatter.17.cloned.1.call-update) | async-done | bytes 6275248 | tf_op jit(solution)/shard_map/reduce_scatter | solution.py:71
  665.5 154.3 %reduce-scatter.13.cloned.1.call-done = bf16[4,729,1076]{1,2,0:T(8,128)(2,1)} async-done(((bf16[8,729,1076]{1,2,0:T(8,128)(2,1)}), bf16[4,729,1076]{1,2,0:T(8,128)(2,1)}) %reduce-scatter.13.cloned.1.call-update) | async-done | bytes 6275248 | tf_op jit(solution)/shard_map/reduce_scatter | solution.py:47
  819.8 17.1 fusion.104
  837.5 159.6 %all-gather.17.cloned.1.call-done = bf16[8,729,1076]{1,2,0:T(8,128)(2,1)} async-done(((bf16[4,729,1076]{1,2,0:T(8,128)(2,1)}), bf16[8,729,1076]{1,2,0:T(8,128)(2,1)}) %all-gather.17.cloned.1.call-update) | async-done | bytes 12550480 | tf_op jit(solution)/shard_map/all_gather | solution.py:90
  997.1 15.9 convolution_convert_fusion.2
  1013.4 145.1 %all-gather.15.cloned.1.call-done = bf16[8,729,1076]{1,2,0:T(8,128)(2,1)} async-done(((bf16[4,729,1076]{1,2,0:T(8,128)(2,1)}), bf16[8,729,1076]{1,2,0:T(8,128)(2,1)}) %all-gather.15.cloned.1.call-update) | async-done | bytes 12550480 | tf_op jit(solution)/shard_map/all_gather | solution.py:58
  1158.5 15.9 convolution_convert_fusion.3
  1174.5 50.8 %reduce-scatter.19.cloned.1.call-done = bf16[2,729,576]{1,2,0:T(8,128)(2,1)} async-done(((bf16[8,729,576]{1,2,0:T(8,128)(2,1)}), bf16[2,729,576]{1,2,0:T(8,128)(2,1)}) %reduce-scatter.19.cloned.1.call-update) | async-done | bytes 1679632 | tf_op jit(solution)/shard_map/reduce_scatter | solution.py:98
  1225.3 4.7 all-to-all-start.5
  1230.7 61.2 %reduce-scatter.15.cloned.1.call-done = bf16[2,729,576]{1,2,0:T(8,128)(2,1)} async-done(((bf16[8,729,576]{1,2,0:T(8,128)(2,1)}), bf16[2,729,576]{1,2,0:T(8,128)(2,1)}) %reduce-scatter.15.cloned.1.call-update) | async-done | bytes 1679632 | tf_op jit(solution)/shard_map/reduce_scatter | solution.py:63
  1291.9 4.7 all-to-all-start.3
  1296.7 2.9 fusion.60
  1300.2 3.4 fusion.67
  1304.2 13.9 all-to-all-done.3
  1320.2 5.1 fusion.106
  1327.5 24.0 %all_to_all.62 = bf16[2,1,729,576]{2,3,1,0:T(8,128)(2,1)} all-to-all(bf16[2,1,729,576]{2,3,1,0:T(8,128)(2,1)S(1)} %pad_maximum_fusion.4), channel_id=1, replica_groups=mesh['dp'=4,'row'=2,'col'=4] {'row'}, dimensions={0} | all-to-all | bytes 3359232 | tf_op jit(solution)/shard_map/all_to_all | solution.py:34
  1351.6 50.0 %all-gather.27.cloned.1.call-done = bf16[8,1,729,576]{2,3,1,0:T(8,128)(2,1)} async-done(((bf16[2,1,729,576]{2,3,1,0:T(8,128)(2,1)}), bf16[8,1,729,576]{2,3,1,0:T(8,128)(2,1)}) %all-gather.27.cloned.1.call-update) | async-done | bytes 6718480 | tf_op jit(solution)/shard_map/all_gather | solution.py:36
  1401.6 7.4 fusion.84
  1409.3 47.6 %reduce-scatter.21.cloned.1.call-done = bf16[4,729,288]{1,2,0:T(8,128)(2,1)} async-done(((bf16[8,729,288]{1,2,0:T(8,128)(2,1)}), bf16[4,729,288]{1,2,0:T(8,128)(2,1)}) %reduce-scatter.21.cloned.1.call-update) | async-done | bytes 1679632 | tf_op jit(solution)/shard_map/reduce_scatter | solution.py:71
  1457.0 70.3 %while.27 = (s32[]{:T(128)}, f32[4,729,288]{1,2,0:T(8,128)}, bf16[4,729,288]{1,2,0:T(8,128)(2,1)}, f32[4,729,288]{1,2,0:T(8,128)S(1)}, bf16[4,729,288]{1,2,0:T(8...) while((s32[]{:T(128)}, f32[4,729,288]{1,2,0:T(8,128)}, ...), condition=%wide.region_18.19_spmd, body=%wide.region_17.18_spmd.sunk | while | flops 1549022848 | bytes 52812796 | solution.py:175
  1464.5 2.6 fusion.164
  1467.1 3.2 multiply_convert_fusion.3
  1484.7 3.2 multiply_convert_fusion.3
  1502.3 3.2 multiply_convert_fusion.3
  1517.2 2.6 fusion.164
  1519.8 3.2 multiply_convert_fusion.3
  1527.2 3.9 fusion.108
  1531.2 3.4 pad_maximum_fusion
  1534.6 7.8 copy.117
  1542.4 130.3 %all-gather.19.cloned.1.call-done = bf16[8,729,864]{2,1,0:T(8,128)(2,1)} async-done(((bf16[4,729,864]{2,1,0:T(8,128)(2,1)}), bf16[8,729,864]{2,1,0:T(8,128)(2,1)}) %all-gather.19.cloned.1.call-update) | async-done | bytes 10077712 | tf_op jit(solution)/shard_map/all_gather | solution.py:90
  1672.7 13.7 convolution_convert_fusion.4
  1686.7 14.8 fusion.81
  1701.5 15.1 fusion.78
  1716.6 7.8 fusion.96
  1724.4 10.2 bitcast_convert_fusion
  1736.1 14.7 reduce-scatter.23.cloned.1.call-done
  1750.8 4.7 all-to-all-start.7
  1758.9 156.0 %all-reduce.4.cloned.1.call-done = (bf16[576,288]{1,0:T(8,128)(2,1)}, bf16[576,288]{1,0:T(8,128)(2,1)}, bf16[576,288]{1,0:T(8,128)(2,1)}, bf16[288,576]{1,0:T(8,...) async-done(((bf16[576,288]{1,0:T(8,128)(2,1)}, bf16[576,288]{1,0:T(8,128)(2,1)}, bf16[576,288]{1,0:T(8,128)(2,1)}, bf16[288,576]{1,0:T(8,128)(2,1)}, ...) | async-done | bytes 3806224 | tf_op jit(solution)/shard_map/psum | solution.py:320
  1928.1 2.9 fusion.54
  1931.0 41.5 %all-reduce = (f32[1152]{0:T(1024)}, f32[1152]{0:T(1024)}, f32[1152]{0:T(1024)S(1)}, f32[1152]{0:T(1024)S(1)}, f32[1152]{0:T(1024)}, /*index=5*/f32[1152]{0:T(10...) all-reduce(f32[1152]{0:T(1024)S(1)} %get-tuple-element.243, ...), channel_id=1, replica_groups=mesh['dp'=4,'row'=2,'col'=4] {'dp','row','col'}, use_global_device_ids=true, to_apply=%region_23.24 | all-reduce | flops 13520 | bytes 108160 | tf_op jit(solution)/shard_map/psum | solution.py:299
  1973.8 5.1 fusion.53
  1979.0 3.8 copy.119
  (255 shorter events, 127.1 us)
Async XLA Ops:
  7.2 504.0 %copy-start = (bf16[576,1076]{1,0:T(8,128)(2,1)S(1)}, bf16[576,1076]{1,0:T(8,128)(2,1)}, u32[]{:S(2)}) copy-start(bf16[576,1076]{1,0:T(8,128)(2,1)} %param.34) | copy-start | bytes 3718660
  7.2 4.0 copy-start.18
  7.2 3.9 copy-start.31
  7.2 82.7 %all-gather.21.cloned.1.call-start = ((), (), s32[]{:S(2)}) async-start(), calls=%async_computation.28 | async-start | bytes 8847360 | tf_op jit(solution)/shard_map/all_gather | solution.py:36
  10.0 422.0 %copy-start.2 = (bf16[1,729,1152]{1,2,0:T(8,128)(2,1)}, bf16[1,729,1152]{1,2,0:T(8,128)(2,1)S(1)}, u32[]{:S(2)}) copy-start(bf16[1,729,1152]{1,2,0:T(8,128)(2,1)S(1)} %copy.104) | copy-start | bytes 5038852
  10.5 0.6 copy-start.20
  10.6 0.6 copy-start.22
  38.3 188.9 %reduce-scatter.9.cloned.1.call-start = ((), (), s32[]{:S(2)}) async-start(), calls=%async_computation.16 | async-start | bytes 15826944 | tf_op jit(solution)/shard_map/reduce_scatter | solution.py:47
  39.6 64.8 %copy-start.12 = (bf16[576,288]{1,0:T(8,128)(2,1)}, bf16[576,288]{1,0:T(8,128)(2,1)S(1)}, u32[]{:S(2)}) copy-start(bf16[576,288]{1,0:T(8,128)(2,1)S(1)} %copy.105) | copy-start | bytes 995332
  104.5 228.9 %all-gather.13.cloned.1.call-start = ((), (), s32[]{:S(2)}) async-start(), calls=%async_computation.17 | async-start | bytes 5308416 | tf_op jit(solution)/shard_map/all_gather | solution.py:58
  235.8 3.2 copy-start.36
  235.8 3.2 copy-start.37
  250.5 82.9 %copy-start.39 = (bf16[288,576]{1,0:T(8,128)(2,1)S(1)}, bf16[288,576]{1,0:T(8,128)(2,1)}, u32[]{:S(2)}) copy-start(bf16[288,576]{1,0:T(8,128)(2,1)} %param.30) | copy-start | bytes 995332
  283.9 122.7 %reduce-scatter.11.cloned.1.call-start = ((), (), s32[]{:S(2)}) async-start(), calls=%async_computation.18 | async-start | bytes 8847360 | tf_op jit(solution)/shard_map/reduce_scatter | solution.py:63
  342.2 117.1 %all-gather.25.cloned.1.call-start = ((), (), s32[]{:S(2)}) async-start(), calls=%async_computation.30 | async-start | bytes 8847360 | tf_op jit(solution)/shard_map/all_gather | solution.py:36
  372.6 138.5 %all-gather.23.cloned.1.call-start = ((), (), s32[]{:S(2)}) async-start(), calls=%async_computation.29 | async-start | bytes 8847360 | tf_op jit(solution)/shard_map/all_gather | solution.py:36
  431.7 0.7 copy-start.35
  432.4 0.8 copy-start.17
  432.4 0.8 copy-start.32
  433.2 1.7 copy-start.4
  435.1 24.3 %copy-start.38 = (bf16[1076,576]{0,1:T(8,128)(2,1)S(1)}, bf16[1076,576]{0,1:T(8,128)(2,1)}, u32[]{:S(2)}) copy-start(bf16[1076,576]{0,1:T(8,128)(2,1)} %param.36) | copy-start | bytes 3718660
  459.3 206.1 %reduce-scatter.17.cloned.1.call-start = ((), (), s32[]{:S(2)}) async-start(), calls=%async_computation.22 | async-start | bytes 19906560 | tf_op jit(solution)/shard_map/reduce_scatter | solution.py:71
  476.0 343.7 %reduce-scatter.13.cloned.1.call-start = ((), (), s32[]{:S(2)}) async-start(), calls=%async_computation.19 | async-start | bytes 19906560 | tf_op jit(solution)/shard_map/reduce_scatter | solution.py:47
  527.7 292.0 %copy-start.33 = (f32[1076]{0:T(1024)S(1)}, f32[1076]{0:T(1024)}, u32[]{:S(2)}) copy-start(f32[1076]{0:T(1024)} %param.35) | copy-start | bytes 12916
  527.8 469.3 %all-gather.17.cloned.1.call-start = ((), (), s32[]{:S(2)}) async-start(), calls=%async_computation.23 | async-start | bytes 19906560 | tf_op jit(solution)/shard_map/all_gather | solution.py:90
  836.8 321.7 %all-gather.15.cloned.1.call-start = ((), (), s32[]{:S(2)}) async-start(), calls=%async_computation.20 | async-start | bytes 19906560 | tf_op jit(solution)/shard_map/all_gather | solution.py:58
  837.4 387.9 %reduce-scatter.19.cloned.1.call-start = ((), (), s32[]{:S(2)}) async-start(), calls=%async_computation.24 | async-start | bytes 8847360 | tf_op jit(solution)/shard_map/reduce_scatter | solution.py:98
  1013.0 279.0 %reduce-scatter.15.cloned.1.call-start = ((), (), s32[]{:S(2)}) async-start(), calls=%async_computation.21 | async-start | bytes 8847360 | tf_op jit(solution)/shard_map/reduce_scatter | solution.py:63
  1225.3 66.6 %all-to-all-start.5 = ((bf16[2,729,576]{1,2,0:T(8,128)(2,1)}), bf16[2,729,576]{1,2,0:T(8,128)(2,1)}, u32[]{:S(2)}, u32[]{:S(2)}) async-start(bf16[2,729,576]{1,2,0:T(8,128)(2,1)} %reduce-scatter.19.cloned.1.call-done), calls=%async_computation.11 | async-start | bytes 3538944 | tf_op jit(solution)/shard_map/all_to_all | solution.py:40
  1230.0 70.2 %copy-start.5 = (f32[1,729,1152]{1,2,0:T(8,128)S(1)}, f32[1,729,1152]{1,2,0:T(8,128)}, u32[]{:S(2)}) copy-start(f32[1,729,1152]{1,2,0:T(8,128)} %copy-done.4) | copy-start | bytes 10077700
  1291.9 26.2 %all-to-all-start.3 = ((bf16[2,729,576]{1,2,0:T(8,128)(2,1)}), bf16[2,729,576]{1,2,0:T(8,128)(2,1)}, u32[]{:S(2)}, u32[]{:S(2)}) async-start(bf16[2,729,576]{1,2,0:T(8,128)(2,1)} %reduce-scatter.15.cloned.1.call-done), calls=%async_computation.7 | async-start | bytes 3538944 | tf_op jit(solution)/shard_map/all_to_all | solution.py:40
  1296.7 105.0 %all-gather.27.cloned.1.call-start = ((), (), s32[]{:S(2)}) async-start(), calls=%async_computation.31 | async-start | bytes 8847360 | tf_op jit(solution)/shard_map/all_gather | solution.py:36
  1318.2 2.0 copy-start.7
  1318.2 2.0 copy-start.29
  1318.2 2.0 copy-start.30
  1318.2 2.0 copy-start.34
  1325.2 1.7 copy-start.6
  1327.5 74.2 %copy-start.40 = (bf16[288,576]{1,0:T(8,128)(2,1)S(1)}, bf16[288,576]{1,0:T(8,128)(2,1)}, u32[]{:S(2)}) copy-start(bf16[288,576]{1,0:T(8,128)(2,1)} %param.30) | copy-start | bytes 995332
  1351.5 105.4 %reduce-scatter.21.cloned.1.call-start = ((), (), s32[]{:S(2)}) async-start(), calls=%async_computation.25 | async-start | bytes 5308416 | tf_op jit(solution)/shard_map/reduce_scatter | solution.py:71
  1409.1 263.7 %all-gather.19.cloned.1.call-start = ((), (), s32[]{:S(2)}) async-start(), calls=%async_computation.26 | async-start | bytes 15826944 | tf_op jit(solution)/shard_map/all_gather | solution.py:90
  1527.2 3.9 copy-start.9
  1542.3 130.4 %copy-start.13 = (bf16[576,288]{1,0:T(8,128)(2,1)S(1)}, bf16[576,288]{1,0:T(8,128)(2,1)}, u32[]{:S(2)}) copy-start(bf16[576,288]{1,0:T(8,128)(2,1)} %copy-done.12) | copy-start | bytes 995332
  1542.3 130.4 %copy-start.14 = (bf16[576,288]{1,0:T(8,128)(2,1)S(1)}, bf16[576,288]{1,0:T(8,128)(2,1)}, u32[]{:S(2)}) copy-start(bf16[576,288]{1,0:T(8,128)(2,1)} %copy.106) | copy-start | bytes 995332
  1542.3 130.4 %copy-start.15 = (bf16[576,288]{1,0:T(8,128)(2,1)S(1)}, bf16[576,288]{1,0:T(8,128)(2,1)}, u32[]{:S(2)}) copy-start(bf16[576,288]{1,0:T(8,128)(2,1)} %copy.107) | copy-start | bytes 995332
  1542.4 208.4 %reduce-scatter.23.cloned.1.call-start = ((), (), s32[]{:S(2)}) async-start(), calls=%async_computation.27 | async-start | bytes 8847360 | tf_op jit(solution)/shard_map/reduce_scatter | solution.py:98
  1686.4 228.5 %all-reduce.4.cloned.1.call-start = ((), (), s32[]{:S(2)}) async-start(), calls=%async_computation.32 | async-start | bytes 8699904 | tf_op jit(solution)/shard_map/psum | solution.py:320
  1686.7 37.7 %slice-start = ((s8[10551296]{0:T(1024)(128)(4,1)}), s8[4194304]{0:T(1024)(128)(4,1)S(1)}, s32[]{:S(2)}) async-start(s8[10551296]{0:T(1024)(128)(4,1)} %bitcast.284), calls=%async_computation.33 | async-start | bytes 8388608
  1686.7 37.7 %slice-start.1 = ((s8[10551296]{0:T(1024)(128)(4,1)}), s8[4194304]{0:T(1024)(128)(4,1)S(1)}, s32[]{:S(2)}) async-start(s8[10551296]{0:T(1024)(128)(4,1)} %bitcast.284), calls=%async_computation.34 | async-start | bytes 8388608
  1701.5 22.8 %slice-start.2 = ((s8[10551296]{0:T(1024)(128)(4,1)}), s8[2162688]{0:T(1024)(128)(4,1)S(1)}, s32[]{:S(2)}) async-start(s8[10551296]{0:T(1024)(128)(4,1)} %bitcast.284), calls=%async_computation.35 | async-start | bytes 4325376
  1736.0 19.4 copy-start.19
  1736.1 19.5 copy-start.24
  1736.1 20.1 %copy-start.28 = (f32[2,576]{1,0:T(2,128)S(1)}, f32[2,576]{1,0:T(2,128)}, u32[]{:S(2)}) copy-start(f32[2,576]{1,0:T(2,128)} %get-tuple-element.247) | copy-start | bytes 13828
  1736.1 20.2 %copy-start.8 = (bf16[1,729,1152]{1,2,0:T(8,128)(2,1)S(1)}, bf16[1,729,1152]{1,2,0:T(8,128)(2,1)}, u32[]{:S(2)}) copy-start(bf16[1,729,1152]{1,2,0:T(8,128)(2,1)} %get-tuple-element.320) | copy-start | bytes 5038852
  1750.8 174.9 %all-to-all-start.7 = ((bf16[2,729,576]{1,2,0:T(8,128)(2,1)}), bf16[2,729,576]{1,2,0:T(8,128)(2,1)}, u32[]{:S(2)}, u32[]{:S(2)}) async-start(bf16[2,729,576]{1,2,0:T(8,128)(2,1)} %reduce-scatter.23.cloned.1.call-done), calls=%async_computation.15 | async-start | bytes 3538944 | tf_op jit(solution)/shard_map/all_to_all | solution.py:40
  1914.9 6.4 copy-start.16
  1914.9 7.3 copy-start.11
  1917.1 6.8 copy-start.10
  1923.9 4.2 copy-start.3
  1923.9 4.2 copy-start.21
  1923.9 4.2 copy-start.23
  1925.6 5.4 copy-start.25
  1925.6 5.4 copy-start.26
  1925.6 5.4 copy-start.27
  1973.8 9.6 copy-start.1
Sparse Core Ops, SparseCore 0:
  38.5 51.3 all-gather.20
  104.6 122.6 reduce-scatter.8
  284.0 49.3 all-gather.12
  342.4 64.1 reduce-scatter.10
  408.0 50.8 all-gather.24
  460.3 50.8 all-gather.22
  513.5 151.9 reduce-scatter.16
  667.8 151.9 reduce-scatter.12
  837.0 160.0 all-gather.16
  998.5 160.0 all-gather.14
  1161.1 64.1 reduce-scatter.18
  1227.7 64.1 reduce-scatter.14
  1351.7 49.9 all-gather.26
  1409.2 47.7 reduce-scatter.20
  1542.5 130.1 all-gather.18
  1686.5 64.1 reduce-scatter.22
  1754.6 160.2 all-reduce.3
